TPU v7x, 32 devices: a whole 2x2x4 slice. The times are simulated.
32 devices in a mesh: groups: 2 (over x), expert: 16 (over z, y, core).
Axes of the slice: x: 2, y: 2, z: 4, core: 2. Of those that a mesh axis runs over, the one named last changes fastest.
Arguments:
- tokens: bfloat16 [128, 6144], P(('groups', 'expert')), parts along dimension 0, may hold values from -64 to 64
- router_weight: bfloat16 [12288, 4], P('groups'), parts along dimension 0, may hold values from -1 to 1
- expert_ids: int32 [128, 2], P(('groups', 'expert')), parts along dimension 0, may hold values from 0 to 3, as said below
- slots: int32 [128, 2], P(('groups', 'expert')), parts along dimension 0, may hold values from 0 to 3, as said below
- gate_weight: bfloat16 [6144, 32768], P(None, 'expert'), may hold values from -0.078125 to 0.078125
- up_weight: bfloat16 [6144, 32768], P(None, 'expert'), may hold values from -0.078125 to 0.078125
- down_weight: bfloat16 [32768, 6144], P('expert'), may hold values from -0.0625 to 0.0625
Outputs:
- mixed_rows: bfloat16 [128, 6144], P(('groups', 'expert')), parts along dimension 0
- balance: float32 [2], P('groups'), parts along dimension 0
There are 2 independent parts, one for each index of `groups`. A program takes and returns all parts, laid end to end along the dimension named above; an argument that names none is the same for every part. Nothing has to cross between parts.
Inputs may be any that keep to these rules, and one draw needn't show every extreme that they name: `expert_ids`: each row names two different experts; one expert, drawn from the seed, is named by every token. Within the rows of one device the slots of the assignments to one expert are distinct; on every device exactly 2 assignments of the expert that every token names have slots below 2, and no expert has more.
All inputs are finite; a program needn't handle non-finite values.
Results may differ from a plain program's by a relative error of at most 0.0058.
Values may be sent and summed in bfloat16 or wider, within the bound.
A program may use at most 128 MiB of HBM per device.

v0:
```python
import functools

import jax
import jax.numpy as jnp
from jax import lax
from jax.experimental import pallas as pl
from jax.experimental.pallas import tpu as pltpu
from jax.sharding import PartitionSpec as P

EXPERTS = 4
CAP = 2
MESH = pl.DeviceIdType.MESH
F32 = jnp.float32
BF16 = jnp.bfloat16

X_PARTS = 3
K_STEPS = 6
W_SLOTS = 4
D_PARTS = 6
D_AHEAD = 1


def each(low, high, body):
    if high - low <= 16:
        for index in range(low, high):
            body(index)
    else:

        def step(index, carry):
            body(index)
            return carry

        lax.fori_loop(low, high, step, 0)


def kernel(
    n,
    tok_hbm,
    rw_hbm,
    ids_hbm,
    slots_hbm,
    gate_hbm,
    up_hbm,
    down_hbm,
    out_hbm,
    bal_hbm,
    tok_ref,
    rw_ref,
    ids_ref,
    slots_ref,
    out_ref,
    bal_ref,
    gate_buf,
    up_buf,
    down_buf,
    send_x,
    x_buf,
    acc_g,
    acc_u,
    hid,
    part,
    pair,
    summed,
    back,
    weights,
    stat_own,
    stat_in,
    stat_pair,
    gate_sem,
    up_sem,
    down_sem,
    xs_sem,
    xr_sem,
    fs_sem,
    fr_sem,
    ps_sem,
    pr_sem,
    bs_sem,
    br_sem,
    ss_sem,
    sr_sem,
    in_sem,
    out_sem,
):
    me = lax.axis_index("expert")
    core = lax.rem(me, 2)
    chip = me // 2
    chips = n // 2
    per_expert = chips // EXPERTS
    partner = me + 1 - 2 * core
    tok_rows, width = tok_ref.shape
    k_rows = width // K_STEPS
    x_cols = width // X_PARTS
    d_cols = width // D_PARTS
    steps_per_part = K_STEPS // X_PARTS

    def chip_at(offset):
        return lax.rem(chip + offset, chips)

    def same_core(offset):
        return {"expert": chip_at(offset) * 2 + core}

    def weight_copies(k):
        slot = lax.rem(k, W_SLOTS)
        rows = pl.ds(k * k_rows, k_rows)
        return (
            pltpu.make_async_copy(gate_hbm.at[rows], gate_buf.at[slot], gate_sem.at[slot]),
            pltpu.make_async_copy(up_hbm.at[rows], up_buf.at[slot], up_sem.at[slot]),
        )

    def down_copy(j):
        cols = pl.ds(pl.multiple_of(j * d_cols, 128), d_cols)
        return pltpu.make_async_copy(down_hbm.at[:, cols], down_buf.at[j], down_sem.at[j])

    inputs = [
        pltpu.make_async_copy(source, target, in_sem.at[i])
        for i, (source, target) in enumerate(
            (
                (tok_hbm, tok_ref),
                (ids_hbm, ids_ref),
                (slots_hbm, slots_ref),
                (rw_hbm, rw_ref),
            )
        )
    ]
    for copy in inputs:
        copy.start()
    barrier = pltpu.get_barrier_semaphore()
    each(
        1,
        chips,
        lambda o: pl.semaphore_signal(barrier, inc=1, device_id=same_core(o), device_id_type=MESH),
    )
    pl.semaphore_signal(barrier, inc=1, device_id={"expert": partner}, device_id_type=MESH)

    for copy in inputs:
        copy.wait()
    for k in range(W_SLOTS):
        for copy in weight_copies(jnp.int32(k)):
            copy.start()
    for j in range(D_AHEAD):
        down_copy(j).start()

    tok = tok_ref[...].astype(F32)
    ids = [[ids_ref[k, t] for k in range(2)] for t in range(tok_rows)]
    cells = [
        [
            jnp.where(slots_ref[k, t] < CAP, ids_ref[k, t] * CAP + slots_ref[k, t], -1)
            for k in range(2)
        ]
        for t in range(tok_rows)
    ]
    slot_of = lax.broadcasted_iota(jnp.int32, (CAP, width), 0)
    for e in range(EXPERTS):
        rows = jnp.zeros((CAP, width), F32)
        for t in range(tok_rows):
            for k in range(2):
                hit = slot_of + e * CAP == cells[t][k]
                rows = jnp.where(hit, jnp.broadcast_to(tok[t : t + 1], (CAP, width)), rows)
        send_x[e] = rows.astype(BF16)

    pl.semaphore_wait(barrier, chips)

    def x_cols_of(a):
        return pl.ds(pl.multiple_of(a * x_cols, 128), x_cols)

    def x_send(a, offset):
        return pltpu.make_async_remote_copy(
            src_ref=send_x.at[chip_at(offset) // per_expert, :, x_cols_of(a)],
            dst_ref=x_buf.at[core * chips + chip, :, x_cols_of(a)],
            send_sem=xs_sem.at[a],
            recv_sem=xr_sem.at[a],
            device_id=same_core(offset),
            device_id_type=MESH,
        )

    def x_own(a):
        return pltpu.make_async_copy(
            send_x.at[chip // per_expert, :, x_cols_of(a)],
            x_buf.at[core * chips + chip, :, x_cols_of(a)],
            xr_sem.at[a],
        )

    def x_wait(a):
        half = x_buf.at[pl.ds(core * chips, chips), :, x_cols_of(a)]
        pltpu.make_async_copy(half, half, xr_sem.at[a]).wait()

    def x_forward(a):
        half = x_buf.at[pl.ds(core * chips, chips), :, x_cols_of(a)]
        return pltpu.make_async_remote_copy(
            src_ref=half,
            dst_ref=half,
            send_sem=fs_sem.at[a],
            recv_sem=fr_sem.at[a],
            device_id={"expert": partner},
            device_id_type=MESH,
        )

    for a in range(X_PARTS):
        each(1, chips, lambda o, a=a: x_send(a, o).start())
        x_own(a).start()

    lane = lax.broadcasted_iota(jnp.int32, (tok_rows, 128), 1)
    row = lax.broadcasted_iota(jnp.int32, (tok_rows, 128), 0)
    logits = jnp.zeros((tok_rows, 128), F32)
    for e in range(EXPERTS):
        dots = jnp.sum(tok * rw_ref[e : e + 1, :].astype(F32), axis=1, keepdims=True)
        logits = jnp.where(lane == e, dots, logits)
    real = lane < EXPERTS
    top = jnp.max(jnp.where(real, logits, -jnp.inf), axis=1, keepdims=True)
    raised = jnp.where(real, jnp.exp(jnp.where(real, logits - top, 0.0)), 0.0)
    probs = raised / jnp.sum(raised, axis=1, keepdims=True)

    def column(values):
        result = jnp.zeros((tok_rows, 128), jnp.int32)
        for t in range(tok_rows):
            result = jnp.where(row == t, values[t], result)
        return result

    chosen = []
    for k in range(2):
        named = lane == column([ids[t][k] for t in range(tok_rows)])
        chosen.append(jnp.sum(jnp.where(named, logits, 0.0), axis=1, keepdims=True))
    top_two = jnp.maximum(chosen[0], chosen[1])
    lifted = [jnp.exp(value - top_two) for value in chosen]
    mix = jnp.zeros((tok_rows, 128), F32)
    for k in range(2):
        cell = column([cells[t][k] for t in range(tok_rows)])
        gate = lifted[k] / (lifted[0] + lifted[1])
        mix = mix + jnp.where(lane == cell, gate, 0.0)
    weights[...] = mix
    counts = jnp.zeros((tok_rows, 128), F32)
    for t in range(tok_rows):
        for k in range(2):
            counts = counts + jnp.where(lane == ids[t][k], 1.0, 0.0)
    stat_own[...] = jnp.zeros((8, 128), F32)
    stat_own[0:1] = counts[0:1]
    stat_own[1:2] = jnp.sum(probs, axis=0, keepdims=True)

    def stat_send(offset):
        return pltpu.make_async_remote_copy(
            src_ref=stat_own,
            dst_ref=stat_in.at[chip],
            send_sem=ss_sem.at[0],
            recv_sem=sr_sem.at[0],
            device_id=same_core(offset),
            device_id_type=MESH,
        )

    def stat_swap():
        return pltpu.make_async_remote_copy(
            src_ref=stat_pair.at[0],
            dst_ref=stat_pair.at[1],
            send_sem=ss_sem.at[1],
            recv_sem=sr_sem.at[1],
            device_id={"expert": partner},
            device_id_type=MESH,
        )

    each(1, chips, lambda o: stat_send(o).start())
    stat_mine = pltpu.make_async_copy(stat_own, stat_in.at[chip], sr_sem.at[0])
    stat_mine.start()

    acc_g[...] = jnp.zeros(acc_g.shape, F32)
    acc_u[...] = jnp.zeros(acc_u.shape, F32)

    x_wait(0)
    x_forward(0).start()

    def k_step(k, carry):
        a = k // steps_per_part
        within = lax.rem(k, steps_per_part)

        @pl.when(within == 0)
        def _():
            x_forward(a).wait_recv()

        slot = lax.rem(k, W_SLOTS)
        gate_copy, up_copy = weight_copies(k)
        cols = pl.ds(pl.multiple_of(k * k_rows, 128), k_rows)
        x = x_buf[:, :, cols].reshape(n * CAP, k_rows)
        gate_copy.wait()
        acc_g[...] += jnp.dot(x, gate_buf[slot], preferred_element_type=F32)
        up_copy.wait()
        acc_u[...] += jnp.dot(x, up_buf[slot], preferred_element_type=F32)

        @pl.when(k + W_SLOTS < K_STEPS)
        def _():
            for copy in weight_copies(k + W_SLOTS):
                copy.start()

        @pl.when(k + D_AHEAD < D_PARTS)
        def _():
            down_copy(k + D_AHEAD).start()

        @pl.when((within == steps_per_part // 2 - 1) & (a + 1 < X_PARTS))
        def _():
            x_wait(a + 1)
            x_forward(a + 1).start()

        return carry

    lax.fori_loop(0, K_STEPS, k_step, 0)

    hid[...] = (jax.nn.silu(acc_g[...]) * acc_u[...]).astype(BF16)

    pltpu.make_async_copy(stat_in, stat_in, sr_sem.at[0]).wait()
    stat_pair[0] = jnp.sum(stat_in[...], axis=0)
    stat_swap().start()

    def d_cols_of(j):
        return pl.ds(pl.multiple_of(j * d_cols, 128), d_cols)

    def pair_send(j):
        return pltpu.make_async_remote_copy(
            src_ref=part.at[pl.ds((1 - core) * chips, chips), :, d_cols_of(j)],
            dst_ref=pair.at[:, :, d_cols_of(j)],
            send_sem=ps_sem.at[j],
            recv_sem=pr_sem.at[j],
            device_id={"expert": partner},
            device_id_type=MESH,
        )

    def back_send(j, offset):
        return pltpu.make_async_remote_copy(
            src_ref=summed.at[chip_at(offset), :, d_cols_of(j)],
            dst_ref=back.at[chip, :, d_cols_of(j)],
            send_sem=bs_sem.at[j],
            recv_sem=br_sem.at[j],
            device_id=same_core(offset),
            device_id_type=MESH,
        )

    def back_own(j):
        return pltpu.make_async_copy(
            summed.at[chip, :, d_cols_of(j)], back.at[chip, :, d_cols_of(j)], br_sem.at[j]
        )

    def add_pair(j):
        pair_send(j).wait_recv()
        mine = part[pl.ds(core * chips, chips), :, d_cols_of(j)].astype(F32)
        summed[:, :, d_cols_of(j)] = (mine + pair[:, :, d_cols_of(j)].astype(F32)).astype(BF16)
        each(1, chips, lambda o: back_send(j, o).start())
        back_own(j).start()

    def d_step(j, carry):
        down_copy(j).wait()
        value = jnp.dot(hid[...], down_buf[j], preferred_element_type=F32)
        part[:, :, d_cols_of(j)] = value.astype(BF16).reshape(n, CAP, d_cols)
        pair_send(j).start()

        @pl.when(j > 0)
        def _():
            add_pair(j - 1)

        return carry

    lax.fori_loop(0, D_PARTS, d_step, 0)
    add_pair(D_PARTS - 1)

    stat_swap().wait_recv()
    total = stat_pair[0] + stat_pair[1]
    tokens_in_all = float(tok_rows * n)
    terms = (total[0:1] / (2.0 * tokens_in_all)) * (total[1:2] / tokens_in_all)
    bal_ref[...] = jnp.broadcast_to(EXPERTS * jnp.sum(terms, axis=1, keepdims=True), (1, 128))
    bal_out = pltpu.make_async_copy(bal_ref, bal_hbm, out_sem.at[D_PARTS])
    bal_out.start()
    stat_swap().wait_send()
    each(1, chips, lambda o: stat_send(o).wait_send())
    for a in range(X_PARTS):
        each(1, chips, lambda o, a=a: x_send(a, o).wait_send())
        x_forward(a).wait_send()

    def out_copy(j):
        cols = pl.ds(j * d_cols, d_cols)
        return pltpu.make_async_copy(out_ref.at[:, cols], out_hbm.at[:, cols], out_sem.at[j])

    mix_of = [weights[:, c : c + 1] for c in range(EXPERTS * CAP)]
    for j in range(D_PARTS):
        pair_send(j).wait_send()
        each(1, chips, lambda o, j=j: back_send(j, o).wait_send())
        cols = pl.ds(j * d_cols, d_cols)
        whole = back.at[:, :, cols]
        pltpu.make_async_copy(whole, whole, br_sem.at[j]).wait()
        mixed = jnp.zeros((tok_rows, d_cols), F32)
        for e in range(EXPERTS):
            value = jnp.sum(
                back[e * per_expert : (e + 1) * per_expert, :, cols].astype(F32), axis=0
            )
            for c in range(CAP):
                mixed = mixed + mix_of[e * CAP + c] * value[c : c + 1]
        out_ref[:, cols] = mixed.astype(BF16)
        out_copy(j).start()
    for j in range(D_PARTS):
        out_copy(j).wait()
    bal_out.wait()


def local(n, tokens, router_weight, expert_ids, slots, gate_weight, up_weight, down_weight):
    tok_rows, width = tokens.shape
    hidden = gate_weight.shape[1]
    chips = n // 2
    k_rows, d_cols = width // K_STEPS, width // D_PARTS
    anywhere = pl.BlockSpec(memory_space=pl.ANY)
    dma = pltpu.SemaphoreType.DMA
    mixed_rows, balance = pl.pallas_call(
        functools.partial(kernel, n),
        out_shape=(
            jax.ShapeDtypeStruct((tok_rows, width), BF16),
            jax.ShapeDtypeStruct((1, 128), F32),
        ),
        in_specs=[anywhere] * 7,
        out_specs=(anywhere, anywhere),
        scratch_shapes=[
            pltpu.VMEM((tok_rows, width), BF16),
            pltpu.VMEM((EXPERTS, width), BF16),
            pltpu.SMEM((2, tok_rows), jnp.int32),
            pltpu.SMEM((2, tok_rows), jnp.int32),
            pltpu.VMEM((tok_rows, width), BF16),
            pltpu.VMEM((1, 128), F32),
            pltpu.VMEM((W_SLOTS, k_rows, hidden), BF16),
            pltpu.VMEM((W_SLOTS, k_rows, hidden), BF16),
            pltpu.VMEM((D_PARTS, hidden, d_cols), BF16),
            pltpu.VMEM((EXPERTS, CAP, width), BF16),
            pltpu.VMEM((n, CAP, width), BF16),
            pltpu.VMEM((n * CAP, hidden), F32),
            pltpu.VMEM((n * CAP, hidden), F32),
            pltpu.VMEM((n * CAP, hidden), BF16),
            pltpu.VMEM((n, CAP, width), BF16),
            pltpu.VMEM((chips, CAP, width), BF16),
            pltpu.VMEM((chips, CAP, width), BF16),
            pltpu.VMEM((chips, CAP, width), BF16),
            pltpu.VMEM((tok_rows, 128), F32),
            pltpu.VMEM((8, 128), F32),
            pltpu.VMEM((chips, 8, 128), F32),
            pltpu.VMEM((2, 8, 128), F32),
            dma((W_SLOTS,)),
            dma((W_SLOTS,)),
            dma((D_PARTS,)),
            dma((X_PARTS,)),
            dma((X_PARTS,)),
            dma((X_PARTS,)),
            dma((X_PARTS,)),
            dma((D_PARTS,)),
            dma((D_PARTS,)),
            dma((D_PARTS,)),
            dma((D_PARTS,)),
            dma((2,)),
            dma((2,)),
            dma((4,)),
            dma((D_PARTS + 1,)),
        ],
        compiler_params=pltpu.CompilerParams(
            collective_id=0, has_side_effects=True, vmem_limit_bytes=67_000_000
        ),
    )(
        tokens,
        router_weight.T,
        expert_ids.T,
        slots.T,
        gate_weight,
        up_weight,
        down_weight,
    )
    return mixed_rows, balance[0, :1]


def solution(mesh):
    in_specs = (
        P(("groups", "expert"), None),
        P("groups", None),
        P(("groups", "expert"), None),
        P(("groups", "expert"), None),
        P(None, "expert"),
        P(None, "expert"),
        P("expert", None),
    )
    out_specs = (P(("groups", "expert"), None), P("groups"))
    return jax.shard_map(
        functools.partial(local, mesh.shape["expert"]),
        mesh=mesh,
        in_specs=in_specs,
        out_specs=out_specs,
        check_vma=False,
    )
```

profile of v0, /device:TPU:0, one launch (start us, length us, event | category | flops | bytes accessed | tf_op | source)
XLA Modules:
  0.0 38.9 jit_solution(8845618003265024672)
XLA Ops:
  0.6 35.1 %shard_map.86 = (bf16[4,6144]{1,0:T(4,128)(2,1)}, f32[1,128]{1,0:T(1,128)}) custom-call(bf16[4,6144]{1,0:T(4,128)(2,1)} %tok_hbm.1, bf16[4,6144]{1,0:T(4,128)(2,1)} %bitcast.5, s32[2,4]{1,0:T(2,128)} %bitcast.6, s32[2,4]{1,0:T(2,128)} %bitcast.7, bf16[6144,2048]{1,0:T(8,128)(2,1)} %gate_hbm.1, bf16[6144,2048]{1,0:T(8,128)(2,1)} %up_hbm.1, ...), custom_call_target="tpu_custom_call" | custom-call | tf_op jit(solution)/shard_map/pallas_call | solution.py:406
  35.8 1.4 %copy.11 = bf16[4,6144]{1,0:T(4,128)(2,1)} copy(bf16[4,6144]{1,0:T(4,128)(2,1)} %get-tuple-element.8) | data formatting | bytes 98304
where the time goes:
time: 39.2 us; the launch traced here: 38.9 us
  Pallas kernels  35.1 us (90%)
  between operations  2.38 us (6%)
  local copies, waits for them, and re-layouts  1.44 us (4%)
    pallas_call x1, Pallas kernels, local(): pl.pallas_call(functools.partial(kernel, n), out_shape=(jax.ShapeDtypeStr...  35.1 us
    unnamed x1, local copies, waits for them, and re-layouts  1.44 us

commit v1 on v0

--- a/solution.py
+++ b/solution.py
@@ -13,11 +13,11 @@
 F32 = jnp.float32
 BF16 = jnp.bfloat16
 
-X_PARTS = 3
 K_STEPS = 6
-W_SLOTS = 4
+W_SLOTS = 5
 D_PARTS = 6
-D_AHEAD = 1
+MAIN_PARTS = 5
+TAIL_PARTS = 2
 
 
 def each(low, high, body):
@@ -42,13 +42,12 @@
     gate_hbm,
     up_hbm,
     down_hbm,
-    out_hbm,
+    out_ref,
     bal_hbm,
     tok_ref,
     rw_ref,
     ids_ref,
     slots_ref,
-    out_ref,
     bal_ref,
     gate_buf,
     up_buf,
@@ -62,6 +61,7 @@
     pair,
     summed,
     back,
+    tail,
     weights,
     stat_own,
     stat_in,
@@ -77,6 +77,8 @@
     pr_sem,
     bs_sem,
     br_sem,
+    ts_sem,
+    tr_sem,
     ss_sem,
     sr_sem,
     in_sem,
@@ -90,9 +92,9 @@
     partner = me + 1 - 2 * core
     tok_rows, width = tok_ref.shape
     k_rows = width // K_STEPS
-    x_cols = width // X_PARTS
     d_cols = width // D_PARTS
-    steps_per_part = K_STEPS // X_PARTS
+    t_cols = d_cols // TAIL_PARTS
+    t_base = MAIN_PARTS * d_cols
 
     def chip_at(offset):
         return lax.rem(chip + offset, chips)
@@ -100,17 +102,28 @@
     def same_core(offset):
         return {"expert": chip_at(offset) * 2 + core}
 
-    def weight_copies(k):
+    def weight_copy(k, source, target, sem):
         slot = lax.rem(k, W_SLOTS)
         rows = pl.ds(k * k_rows, k_rows)
-        return (
-            pltpu.make_async_copy(gate_hbm.at[rows], gate_buf.at[slot], gate_sem.at[slot]),
-            pltpu.make_async_copy(up_hbm.at[rows], up_buf.at[slot], up_sem.at[slot]),
-        )
+        return pltpu.make_async_copy(source.at[rows], target.at[slot], sem.at[slot])
+
+    def gate_copy(k):
+        return weight_copy(k, gate_hbm, gate_buf, gate_sem)
+
+    def up_copy(k):
+        return weight_copy(k, up_hbm, up_buf, up_sem)
 
     def down_copy(j):
         cols = pl.ds(pl.multiple_of(j * d_cols, 128), d_cols)
         return pltpu.make_async_copy(down_hbm.at[:, cols], down_buf.at[j], down_sem.at[j])
+
+    def tail_copy(t):
+        cols = pl.ds(t_base + t * t_cols, t_cols)
+        return pltpu.make_async_copy(
+            down_hbm.at[:, cols],
+            down_buf.at[0, :, pl.ds(t * t_cols, t_cols)],
+            down_sem.at[MAIN_PARTS + t],
+        )
 
     inputs = [
         pltpu.make_async_copy(source, target, in_sem.at[i])
@@ -125,21 +138,22 @@
     ]
     for copy in inputs:
         copy.start()
+    gate_copy(0).start()
     barrier = pltpu.get_barrier_semaphore()
     each(
         1,
-        chips,
-        lambda o: pl.semaphore_signal(barrier, inc=1, device_id=same_core(o), device_id_type=MESH),
+        n,
+        lambda o: pl.semaphore_signal(
+            barrier, inc=1, device_id={"expert": lax.rem(me + o, n)}, device_id_type=MESH
+        ),
     )
-    pl.semaphore_signal(barrier, inc=1, device_id={"expert": partner}, device_id_type=MESH)
 
     for copy in inputs:
         copy.wait()
-    for k in range(W_SLOTS):
-        for copy in weight_copies(jnp.int32(k)):
-            copy.start()
-    for j in range(D_AHEAD):
-        down_copy(j).start()
+    up_copy(0).start()
+    for k in range(1, W_SLOTS):
+        gate_copy(k).start()
+        up_copy(k).start()
 
     tok = tok_ref[...].astype(F32)
     ids = [[ids_ref[k, t] for k in range(2)] for t in range(tok_rows)]
@@ -159,15 +173,15 @@
                 rows = jnp.where(hit, jnp.broadcast_to(tok[t : t + 1], (CAP, width)), rows)
         send_x[e] = rows.astype(BF16)
 
-    pl.semaphore_wait(barrier, chips)
-
-    def x_cols_of(a):
-        return pl.ds(pl.multiple_of(a * x_cols, 128), x_cols)
+    pl.semaphore_wait(barrier, n - 1)
+
+    def k_cols_of(a):
+        return pl.ds(pl.multiple_of(a * k_rows, 128), k_rows)
 
     def x_send(a, offset):
         return pltpu.make_async_remote_copy(
-            src_ref=send_x.at[chip_at(offset) // per_expert, :, x_cols_of(a)],
-            dst_ref=x_buf.at[core * chips + chip, :, x_cols_of(a)],
+            src_ref=send_x.at[chip_at(offset) // per_expert, :, k_cols_of(a)],
+            dst_ref=x_buf.at[core * chips + chip, :, k_cols_of(a)],
             send_sem=xs_sem.at[a],
             recv_sem=xr_sem.at[a],
             device_id=same_core(offset),
@@ -176,17 +190,17 @@
 
     def x_own(a):
         return pltpu.make_async_copy(
-            send_x.at[chip // per_expert, :, x_cols_of(a)],
-            x_buf.at[core * chips + chip, :, x_cols_of(a)],
+            send_x.at[chip // per_expert, :, k_cols_of(a)],
+            x_buf.at[core * chips + chip, :, k_cols_of(a)],
             xr_sem.at[a],
         )
 
     def x_wait(a):
-        half = x_buf.at[pl.ds(core * chips, chips), :, x_cols_of(a)]
+        half = x_buf.at[pl.ds(core * chips, chips), :, k_cols_of(a)]
         pltpu.make_async_copy(half, half, xr_sem.at[a]).wait()
 
     def x_forward(a):
-        half = x_buf.at[pl.ds(core * chips, chips), :, x_cols_of(a)]
+        half = x_buf.at[pl.ds(core * chips, chips), :, k_cols_of(a)]
         return pltpu.make_async_remote_copy(
             src_ref=half,
             dst_ref=half,
@@ -196,7 +210,7 @@
             device_id_type=MESH,
         )
 
-    for a in range(X_PARTS):
+    for a in range(K_STEPS):
         each(1, chips, lambda o, a=a: x_send(a, o).start())
         x_own(a).start()
 
@@ -268,35 +282,28 @@
     x_forward(0).start()
 
     def k_step(k, carry):
-        a = k // steps_per_part
-        within = lax.rem(k, steps_per_part)
-
-        @pl.when(within == 0)
+        @pl.when(k + 1 < K_STEPS)
         def _():
-            x_forward(a).wait_recv()
-
+            x_wait(k + 1)
+            x_forward(k + 1).start()
+
+        x_forward(k).wait_recv()
         slot = lax.rem(k, W_SLOTS)
-        gate_copy, up_copy = weight_copies(k)
         cols = pl.ds(pl.multiple_of(k * k_rows, 128), k_rows)
         x = x_buf[:, :, cols].reshape(n * CAP, k_rows)
-        gate_copy.wait()
+        gate_copy(k).wait()
         acc_g[...] += jnp.dot(x, gate_buf[slot], preferred_element_type=F32)
-        up_copy.wait()
+        up_copy(k).wait()
         acc_u[...] += jnp.dot(x, up_buf[slot], preferred_element_type=F32)
 
         @pl.when(k + W_SLOTS < K_STEPS)
         def _():
-            for copy in weight_copies(k + W_SLOTS):
-                copy.start()
-
-        @pl.when(k + D_AHEAD < D_PARTS)
+            gate_copy(k + W_SLOTS).start()
+            up_copy(k + W_SLOTS).start()
+
+        @pl.when((k >= 1) & (k <= MAIN_PARTS))
         def _():
-            down_copy(k + D_AHEAD).start()
-
-        @pl.when((within == steps_per_part // 2 - 1) & (a + 1 < X_PARTS))
-        def _():
-            x_wait(a + 1)
-            x_forward(a + 1).start()
+            down_copy(k - 1).start()
 
         return carry
 
@@ -349,50 +356,87 @@
         part[:, :, d_cols_of(j)] = value.astype(BF16).reshape(n, CAP, d_cols)
         pair_send(j).start()
 
+        @pl.when(j == 0)
+        def _():
+            for t in range(TAIL_PARTS):
+                tail_copy(t).start()
+
         @pl.when(j > 0)
         def _():
             add_pair(j - 1)
 
         return carry
 
-    lax.fori_loop(0, D_PARTS, d_step, 0)
-    add_pair(D_PARTS - 1)
+    def device_at(offset):
+        return lax.rem(me + offset, n)
+
+    def row_of(device):
+        return lax.rem(device, 2) * chips + device // 2
+
+    def tail_cols(t):
+        return pl.ds(t_base + t * t_cols, t_cols)
+
+    def tail_send(t, offset):
+        return pltpu.make_async_remote_copy(
+            src_ref=part.at[row_of(device_at(offset)), :, tail_cols(t)],
+            dst_ref=tail.at[t, me],
+            send_sem=ts_sem.at[t],
+            recv_sem=tr_sem.at[t],
+            device_id={"expert": device_at(offset)},
+            device_id_type=MESH,
+        )
+
+    def tail_own(t):
+        return pltpu.make_async_copy(
+            part.at[row_of(me), :, tail_cols(t)], tail.at[t, me], tr_sem.at[t]
+        )
+
+    lax.fori_loop(0, MAIN_PARTS, d_step, 0)
+    for t in range(TAIL_PARTS):
+        tail_copy(t).wait()
+        weight = down_buf[0, :, t * t_cols : (t + 1) * t_cols]
+        value = jnp.dot(hid[...], weight, preferred_element_type=F32)
+        part[:, :, tail_cols(t)] = value.astype(BF16).reshape(n, CAP, t_cols)
+        each(1, n, lambda o, t=t: tail_send(t, o).start())
+        tail_own(t).start()
+        if t == 0:
+            add_pair(MAIN_PARTS - 1)
 
     stat_swap().wait_recv()
     total = stat_pair[0] + stat_pair[1]
     tokens_in_all = float(tok_rows * n)
     terms = (total[0:1] / (2.0 * tokens_in_all)) * (total[1:2] / tokens_in_all)
     bal_ref[...] = jnp.broadcast_to(EXPERTS * jnp.sum(terms, axis=1, keepdims=True), (1, 128))
-    bal_out = pltpu.make_async_copy(bal_ref, bal_hbm, out_sem.at[D_PARTS])
+    bal_out = pltpu.make_async_copy(bal_ref, bal_hbm, out_sem.at[0])
     bal_out.start()
     stat_swap().wait_send()
     each(1, chips, lambda o: stat_send(o).wait_send())
-    for a in range(X_PARTS):
+    for a in range(K_STEPS):
         each(1, chips, lambda o, a=a: x_send(a, o).wait_send())
         x_forward(a).wait_send()
 
-    def out_copy(j):
-        cols = pl.ds(j * d_cols, d_cols)
-        return pltpu.make_async_copy(out_ref.at[:, cols], out_hbm.at[:, cols], out_sem.at[j])
-
     mix_of = [weights[:, c : c + 1] for c in range(EXPERTS * CAP)]
-    for j in range(D_PARTS):
+
+    def mix_rows(blocks, cols, per_block):
+        count = per_expert * per_block
+        mixed = jnp.zeros((tok_rows, cols.size), F32)
+        for e in range(EXPERTS):
+            value = jnp.sum(blocks[e * count : (e + 1) * count].astype(F32), axis=0)
+            for c in range(CAP):
+                mixed = mixed + mix_of[e * CAP + c] * value[c : c + 1]
+        out_ref[:, cols] = mixed.astype(BF16)
+
+    for j in range(MAIN_PARTS):
         pair_send(j).wait_send()
         each(1, chips, lambda o, j=j: back_send(j, o).wait_send())
         cols = pl.ds(j * d_cols, d_cols)
         whole = back.at[:, :, cols]
         pltpu.make_async_copy(whole, whole, br_sem.at[j]).wait()
-        mixed = jnp.zeros((tok_rows, d_cols), F32)
-        for e in range(EXPERTS):
-            value = jnp.sum(
-                back[e * per_expert : (e + 1) * per_expert, :, cols].astype(F32), axis=0
-            )
-            for c in range(CAP):
-                mixed = mixed + mix_of[e * CAP + c] * value[c : c + 1]
-        out_ref[:, cols] = mixed.astype(BF16)
-        out_copy(j).start()
-    for j in range(D_PARTS):
-        out_copy(j).wait()
+        mix_rows(back[:, :, cols], cols, 1)
+    for t in range(TAIL_PARTS):
+        pltpu.make_async_copy(tail.at[t], tail.at[t], tr_sem.at[t]).wait()
+        mix_rows(tail[t], tail_cols(t), 2)
+        each(1, n, lambda o, t=t: tail_send(t, o).wait_send())
     bal_out.wait()
 
 
@@ -406,21 +450,20 @@
     mixed_rows, balance = pl.pallas_call(
         functools.partial(kernel, n),
         out_shape=(
-            jax.ShapeDtypeStruct((tok_rows, width), BF16),
+            pltpu.VMEM((tok_rows, width), BF16),
             jax.ShapeDtypeStruct((1, 128), F32),
         ),
         in_specs=[anywhere] * 7,
-        out_specs=(anywhere, anywhere),
+        out_specs=(pl.BlockSpec(memory_space=pltpu.VMEM), anywhere),
         scratch_shapes=[
             pltpu.VMEM((tok_rows, width), BF16),
             pltpu.VMEM((EXPERTS, width), BF16),
             pltpu.SMEM((2, tok_rows), jnp.int32),
             pltpu.SMEM((2, tok_rows), jnp.int32),
-            pltpu.VMEM((tok_rows, width), BF16),
             pltpu.VMEM((1, 128), F32),
             pltpu.VMEM((W_SLOTS, k_rows, hidden), BF16),
             pltpu.VMEM((W_SLOTS, k_rows, hidden), BF16),
-            pltpu.VMEM((D_PARTS, hidden, d_cols), BF16),
+            pltpu.VMEM((MAIN_PARTS, hidden, d_cols), BF16),
             pltpu.VMEM((EXPERTS, CAP, width), BF16),
             pltpu.VMEM((n, CAP, width), BF16),
             pltpu.VMEM((n * CAP, hidden), F32),
@@ -430,28 +473,31 @@
             pltpu.VMEM((chips, CAP, width), BF16),
             pltpu.VMEM((chips, CAP, width), BF16),
             pltpu.VMEM((chips, CAP, width), BF16),
+            pltpu.VMEM((TAIL_PARTS, n, CAP, d_cols // TAIL_PARTS), BF16),
             pltpu.VMEM((tok_rows, 128), F32),
             pltpu.VMEM((8, 128), F32),
             pltpu.VMEM((chips, 8, 128), F32),
             pltpu.VMEM((2, 8, 128), F32),
             dma((W_SLOTS,)),
             dma((W_SLOTS,)),
-            dma((D_PARTS,)),
-            dma((X_PARTS,)),
-            dma((X_PARTS,)),
-            dma((X_PARTS,)),
-            dma((X_PARTS,)),
-            dma((D_PARTS,)),
-            dma((D_PARTS,)),
-            dma((D_PARTS,)),
-            dma((D_PARTS,)),
+            dma((MAIN_PARTS + TAIL_PARTS,)),
+            dma((K_STEPS,)),
+            dma((K_STEPS,)),
+            dma((K_STEPS,)),
+            dma((K_STEPS,)),
+            dma((MAIN_PARTS,)),
+            dma((MAIN_PARTS,)),
+            dma((MAIN_PARTS,)),
+            dma((MAIN_PARTS,)),
+            dma((TAIL_PARTS,)),
+            dma((TAIL_PARTS,)),
             dma((2,)),
             dma((2,)),
             dma((4,)),
-            dma((D_PARTS + 1,)),
+            dma((1,)),
         ],
         compiler_params=pltpu.CompilerParams(
-            collective_id=0, has_side_effects=True, vmem_limit_bytes=67_000_000
+            collective_id=0, has_side_effects=True, vmem_limit_bytes=66_800_000
         ),
     )(
         tokens,

time: 39.2 us -> 35.6 us (0.908)
  Pallas kernels: 35.1 us -> 32.5 us
  local copies, waits for them, and re-layouts: 1.44 us -> 0.62 us
    pallas_call x1, Pallas kernels: 35.1 us -> 32.5 us  [local(): pl.pallas_call(functools.partial(kernel, n), out_shape=(pltpu.VMEM((tok_r...]
    unnamed x1, local copies, waits for them, and re-layouts: 1.44 us -> 0.62 us
where the time goes in v1:
time: 35.6 us; the launch traced here: 35.4 us
  Pallas kernels  32.5 us (91%)
  between operations  2.33 us (7%)
  local copies, waits for them, and re-layouts  0.62 us (2%)
    pallas_call x1, Pallas kernels, local(): pl.pallas_call(functools.partial(kernel, n), out_shape=(pltpu.VMEM((tok_r...  32.5 us

profile of v1, /device:TPU:0, one launch (start us, length us, event | category | flops | bytes accessed | tf_op | source)
XLA Modules:
  0.0 35.4 jit_solution(6442623408934021589)
XLA Ops:
  0.6 32.5 %shard_map.86 = (bf16[4,6144]{1,0:T(4,128)(2,1)S(1)}, f32[1,128]{1,0:T(1,128)}) custom-call(bf16[4,6144]{1,0:T(4,128)(2,1)} %tok_hbm.1, bf16[4,6144]{1,0:T(4,128)(2,1)} %bitcast.5, s32[2,4]{1,0:T(2,128)} %bitcast.6, s32[2,4]{1,0:T(2,128)} %bitcast.7, bf16[6144,2048]{1,0:T(8,128)(2,1)} %gate_hbm.1, bf16[6144,2048]{1,0:T(8,128)(2,1)} %up_hbm.1, ...), custom_call_target="tpu_custom_call" | custom-call | tf_op jit(solution)/shard_map/pallas_call | solution.py:450
  33.1 0.6 %copy.11 = bf16[4,6144]{1,0:T(4,128)(2,1)} copy(bf16[4,6144]{1,0:T(4,128)(2,1)S(1)} %get-tuple-element.6) | data formatting | bytes 98304

commit v2 on v1

--- a/solution.py
+++ b/solution.py
@@ -61,6 +61,7 @@
     pair,
     summed,
     back,
+    tail_out,
     tail,
     weights,
     stat_own,
@@ -320,8 +321,8 @@
 
     def pair_send(j):
         return pltpu.make_async_remote_copy(
-            src_ref=part.at[pl.ds((1 - core) * chips, chips), :, d_cols_of(j)],
-            dst_ref=pair.at[:, :, d_cols_of(j)],
+            src_ref=part.at[1 - core, :, d_cols_of(j)],
+            dst_ref=pair.at[:, d_cols_of(j)],
             send_sem=ps_sem.at[j],
             recv_sem=pr_sem.at[j],
             device_id={"expert": partner},
@@ -345,15 +346,16 @@
 
     def add_pair(j):
         pair_send(j).wait_recv()
-        mine = part[pl.ds(core * chips, chips), :, d_cols_of(j)].astype(F32)
-        summed[:, :, d_cols_of(j)] = (mine + pair[:, :, d_cols_of(j)].astype(F32)).astype(BF16)
+        mine = part[core, :, d_cols_of(j)].astype(F32)
+        both = (mine + pair[:, d_cols_of(j)].astype(F32)).astype(BF16)
+        summed[:, :, d_cols_of(j)] = both.reshape(chips, CAP, d_cols)
         each(1, chips, lambda o: back_send(j, o).start())
         back_own(j).start()
 
     def d_step(j, carry):
         down_copy(j).wait()
         value = jnp.dot(hid[...], down_buf[j], preferred_element_type=F32)
-        part[:, :, d_cols_of(j)] = value.astype(BF16).reshape(n, CAP, d_cols)
+        part[:, :, d_cols_of(j)] = value.astype(BF16).reshape(2, chips * CAP, d_cols)
         pair_send(j).start()
 
         @pl.when(j == 0)
@@ -378,7 +380,7 @@
 
     def tail_send(t, offset):
         return pltpu.make_async_remote_copy(
-            src_ref=part.at[row_of(device_at(offset)), :, tail_cols(t)],
+            src_ref=tail_out.at[t, row_of(device_at(offset))],
             dst_ref=tail.at[t, me],
             send_sem=ts_sem.at[t],
             recv_sem=tr_sem.at[t],
@@ -388,7 +390,7 @@
 
     def tail_own(t):
         return pltpu.make_async_copy(
-            part.at[row_of(me), :, tail_cols(t)], tail.at[t, me], tr_sem.at[t]
+            tail_out.at[t, row_of(me)], tail.at[t, me], tr_sem.at[t]
         )
 
     lax.fori_loop(0, MAIN_PARTS, d_step, 0)
@@ -396,7 +398,7 @@
         tail_copy(t).wait()
         weight = down_buf[0, :, t * t_cols : (t + 1) * t_cols]
         value = jnp.dot(hid[...], weight, preferred_element_type=F32)
-        part[:, :, tail_cols(t)] = value.astype(BF16).reshape(n, CAP, t_cols)
+        tail_out[t] = value.astype(BF16).reshape(n, CAP, t_cols)
         each(1, n, lambda o, t=t: tail_send(t, o).start())
         tail_own(t).start()
         if t == 0:
@@ -433,11 +435,12 @@
         whole = back.at[:, :, cols]
         pltpu.make_async_copy(whole, whole, br_sem.at[j]).wait()
         mix_rows(back[:, :, cols], cols, 1)
+    bal_out.wait()
+    for t in range(TAIL_PARTS):
+        each(1, n, lambda o, t=t: tail_send(t, o).wait_send())
     for t in range(TAIL_PARTS):
         pltpu.make_async_copy(tail.at[t], tail.at[t], tr_sem.at[t]).wait()
         mix_rows(tail[t], tail_cols(t), 2)
-        each(1, n, lambda o, t=t: tail_send(t, o).wait_send())
-    bal_out.wait()
 
 
 def local(n, tokens, router_weight, expert_ids, slots, gate_weight, up_weight, down_weight):
@@ -469,10 +472,11 @@
             pltpu.VMEM((n * CAP, hidden), F32),
             pltpu.VMEM((n * CAP, hidden), F32),
             pltpu.VMEM((n * CAP, hidden), BF16),
-            pltpu.VMEM((n, CAP, width), BF16),
+            pltpu.VMEM((2, chips * CAP, width), BF16),
+            pltpu.VMEM((chips * CAP, width), BF16),
             pltpu.VMEM((chips, CAP, width), BF16),
             pltpu.VMEM((chips, CAP, width), BF16),
-            pltpu.VMEM((chips, CAP, width), BF16),
+            pltpu.VMEM((TAIL_PARTS, n, CAP, d_cols // TAIL_PARTS), BF16),
             pltpu.VMEM((TAIL_PARTS, n, CAP, d_cols // TAIL_PARTS), BF16),
             pltpu.VMEM((tok_rows, 128), F32),
             pltpu.VMEM((8, 128), F32),

time: 35.6 us -> 35.5 us (level)
  no operation moved by 1% of the time
where the time goes in v2:
time: 35.5 us; the launch traced here: 35.4 us
  Pallas kernels  32.4 us (91%)
  between operations  2.33 us (7%)
  local copies, waits for them, and re-layouts  0.62 us (2%)
    pallas_call x1, Pallas kernels, local(): pl.pallas_call(functools.partial(kernel, n), out_shape=(pltpu.VMEM((tok_r...  32.4 us

profile of v2, /device:TPU:0, one launch (start us, length us, event | category | flops | bytes accessed | tf_op | source)
XLA Modules:
  0.0 35.4 jit_solution(5293231955020234205)
XLA Ops:
  0.6 32.4 %shard_map.86 = (bf16[4,6144]{1,0:T(4,128)(2,1)S(1)}, f32[1,128]{1,0:T(1,128)}) custom-call(bf16[4,6144]{1,0:T(4,128)(2,1)} %tok_hbm.1, bf16[4,6144]{1,0:T(4,128)(2,1)} %bitcast.5, s32[2,4]{1,0:T(2,128)} %bitcast.6, s32[2,4]{1,0:T(2,128)} %bitcast.7, bf16[6144,2048]{1,0:T(8,128)(2,1)} %gate_hbm.1, bf16[6144,2048]{1,0:T(8,128)(2,1)} %up_hbm.1, ...), custom_call_target="tpu_custom_call" | custom-call | tf_op jit(solution)/shard_map/pallas_call | solution.py:453
  33.1 0.6 %copy.11 = bf16[4,6144]{1,0:T(4,128)(2,1)} copy(bf16[4,6144]{1,0:T(4,128)(2,1)S(1)} %get-tuple-element.6) | data formatting | bytes 98304

commit v3 on v2

--- a/solution.py
+++ b/solution.py
@@ -43,12 +43,11 @@
     up_hbm,
     down_hbm,
     out_ref,
-    bal_hbm,
+    bal_ref,
     tok_ref,
     rw_ref,
     ids_ref,
     slots_ref,
-    bal_ref,
     gate_buf,
     up_buf,
     down_buf,
@@ -83,7 +82,6 @@
     ss_sem,
     sr_sem,
     in_sem,
-    out_sem,
 ):
     me = lax.axis_index("expert")
     core = lax.rem(me, 2)
@@ -409,8 +407,6 @@
     tokens_in_all = float(tok_rows * n)
     terms = (total[0:1] / (2.0 * tokens_in_all)) * (total[1:2] / tokens_in_all)
     bal_ref[...] = jnp.broadcast_to(EXPERTS * jnp.sum(terms, axis=1, keepdims=True), (1, 128))
-    bal_out = pltpu.make_async_copy(bal_ref, bal_hbm, out_sem.at[0])
-    bal_out.start()
     stat_swap().wait_send()
     each(1, chips, lambda o: stat_send(o).wait_send())
     for a in range(K_STEPS):
@@ -435,12 +431,22 @@
         whole = back.at[:, :, cols]
         pltpu.make_async_copy(whole, whole, br_sem.at[j]).wait()
         mix_rows(back[:, :, cols], cols, 1)
-    bal_out.wait()
     for t in range(TAIL_PARTS):
         each(1, n, lambda o, t=t: tail_send(t, o).wait_send())
     for t in range(TAIL_PARTS):
         pltpu.make_async_copy(tail.at[t], tail.at[t], tr_sem.at[t]).wait()
         mix_rows(tail[t], tail_cols(t), 2)
+
+
+def store(mixed_ref, bal_ref, mixed_hbm, bal_hbm, sem):
+    copies = (
+        pltpu.make_async_copy(mixed_ref, mixed_hbm, sem.at[0]),
+        pltpu.make_async_copy(bal_ref, bal_hbm, sem.at[1]),
+    )
+    for copy in copies:
+        copy.start()
+    for copy in copies:
+        copy.wait()
 
 
 def local(n, tokens, router_weight, expert_ids, slots, gate_weight, up_weight, down_weight):
@@ -454,16 +460,15 @@
         functools.partial(kernel, n),
         out_shape=(
             pltpu.VMEM((tok_rows, width), BF16),
-            jax.ShapeDtypeStruct((1, 128), F32),
+            pltpu.VMEM((1, 128), F32),
         ),
         in_specs=[anywhere] * 7,
-        out_specs=(pl.BlockSpec(memory_space=pltpu.VMEM), anywhere),
+        out_specs=(pl.BlockSpec(memory_space=pltpu.VMEM),) * 2,
         scratch_shapes=[
             pltpu.VMEM((tok_rows, width), BF16),
             pltpu.VMEM((EXPERTS, width), BF16),
             pltpu.SMEM((2, tok_rows), jnp.int32),
             pltpu.SMEM((2, tok_rows), jnp.int32),
-            pltpu.VMEM((1, 128), F32),
             pltpu.VMEM((W_SLOTS, k_rows, hidden), BF16),
             pltpu.VMEM((W_SLOTS, k_rows, hidden), BF16),
             pltpu.VMEM((MAIN_PARTS, hidden, d_cols), BF16),
@@ -498,7 +503,6 @@
             dma((2,)),
             dma((2,)),
             dma((4,)),
-            dma((1,)),
         ],
         compiler_params=pltpu.CompilerParams(
             collective_id=0, has_side_effects=True, vmem_limit_bytes=66_800_000
@@ -511,6 +515,21 @@
         gate_weight,
         up_weight,
         down_weight,
+    )
+    inside = pl.BlockSpec(memory_space=pltpu.VMEM)
+    mixed_rows, balance = pl.pallas_call(
+        store,
+        out_shape=(
+            jax.ShapeDtypeStruct((tok_rows, width), BF16),
+            jax.ShapeDtypeStruct((1, 128), F32),
+        ),
+        in_specs=[inside, inside],
+        out_specs=(anywhere, anywhere),
+        scratch_shapes=[dma((2,))],
+        compiler_params=pltpu.CompilerParams(has_side_effects=True),
+    )(
+        pltpu.with_memory_space_constraint(mixed_rows, pltpu.VMEM),
+        pltpu.with_memory_space_constraint(balance, pltpu.VMEM),
     )
     return mixed_rows, balance[0, :1]
 

time: 35.5 us -> 33.9 us (0.955)
  between operations: 2.33 us -> 0.64 us
  Pallas kernels: 32.4 us -> 33.1 us
  local copies, waits for them, and re-layouts: 0.62 us -> 0 us
    pallas_call x0 -> x1, Pallas kernels: none -> 0.64 us  [local(): pl.pallas_call(store, out_shape=(jax.ShapeDtypeStruct((tok_rows, width),...]
    unnamed x1 -> x0, local copies, waits for them, and re-layouts: 0.62 us -> none
where the time goes in v3:
time: 33.9 us; the launch traced here: 33.7 us
  Pallas kernels  33.1 us (98%)
  between operations  0.64 us (2%)
    pallas_call x1, Pallas kernels, local(): pl.pallas_call(functools.partial(kernel, n), out_shape=(pltpu.VMEM((tok_r...  32.4 us

profile of v3, /device:TPU:0, one launch (start us, length us, event | category | flops | bytes accessed | tf_op | source)
XLA Modules:
  0.0 33.7 jit_solution(16031363828223303048)
XLA Ops:
  0.6 32.4 %shard_map.86 = (bf16[4,6144]{1,0:T(4,128)(2,1)S(1)}, f32[1,128]{1,0:T(1,128)S(1)}) custom-call(bf16[4,6144]{1,0:T(4,128)(2,1)} %tok_hbm.1, bf16[4,6144]{1,0:T(4,128)(2,1)} %bitcast.5, s32[2,4]{1,0:T(2,128)} %bitcast.6, s32[2,4]{1,0:T(2,128)} %bitcast.7, bf16[6144,2048]{1,0:T(8,128)(2,1)} %gate_hbm.1, bf16[6144,2048]{1,0:T(8,128)(2,1)} %up_hbm.1, ...), custom_call_target="tpu_custom_call" | custom-call | tf_op jit(solution)/shard_map/pallas_call | solution.py:459
  33.1 0.6 %shard_map.87 = (bf16[4,6144]{1,0:T(4,128)(2,1)}, f32[1,128]{1,0:T(1,128)}) custom-call(bf16[4,6144]{1,0:T(4,128)(2,1)S(1)} %get-tuple-element.6.mixed_ref, f32[1,128]{1,0:T(1,128)S(1)} %get-tuple-element.7.bal_ref), custom_call_target="tpu_custom_call" | custom-call | tf_op jit(solution)/shard_map/pallas_call | solution.py:520

commit v4 on v3

--- a/solution.py
+++ b/solution.py
@@ -69,17 +69,12 @@
     gate_sem,
     up_sem,
     down_sem,
-    xs_sem,
+    send_sem,
     xr_sem,
-    fs_sem,
     fr_sem,
-    ps_sem,
     pr_sem,
-    bs_sem,
     br_sem,
-    ts_sem,
     tr_sem,
-    ss_sem,
     sr_sem,
     in_sem,
 ):
@@ -181,7 +176,7 @@
         return pltpu.make_async_remote_copy(
             src_ref=send_x.at[chip_at(offset) // per_expert, :, k_cols_of(a)],
             dst_ref=x_buf.at[core * chips + chip, :, k_cols_of(a)],
-            send_sem=xs_sem.at[a],
+            send_sem=send_sem.at[0],
             recv_sem=xr_sem.at[a],
             device_id=same_core(offset),
             device_id_type=MESH,
@@ -203,7 +198,7 @@
         return pltpu.make_async_remote_copy(
             src_ref=half,
             dst_ref=half,
-            send_sem=fs_sem.at[a],
+            send_sem=send_sem.at[0],
             recv_sem=fr_sem.at[a],
             device_id={"expert": partner},
             device_id_type=MESH,
@@ -254,7 +249,7 @@
         return pltpu.make_async_remote_copy(
             src_ref=stat_own,
             dst_ref=stat_in.at[chip],
-            send_sem=ss_sem.at[0],
+            send_sem=send_sem.at[0],
             recv_sem=sr_sem.at[0],
             device_id=same_core(offset),
             device_id_type=MESH,
@@ -264,7 +259,7 @@
         return pltpu.make_async_remote_copy(
             src_ref=stat_pair.at[0],
             dst_ref=stat_pair.at[1],
-            send_sem=ss_sem.at[1],
+            send_sem=send_sem.at[0],
             recv_sem=sr_sem.at[1],
             device_id={"expert": partner},
             device_id_type=MESH,
@@ -321,7 +316,7 @@
         return pltpu.make_async_remote_copy(
             src_ref=part.at[1 - core, :, d_cols_of(j)],
             dst_ref=pair.at[:, d_cols_of(j)],
-            send_sem=ps_sem.at[j],
+            send_sem=send_sem.at[0],
             recv_sem=pr_sem.at[j],
             device_id={"expert": partner},
             device_id_type=MESH,
@@ -331,7 +326,7 @@
         return pltpu.make_async_remote_copy(
             src_ref=summed.at[chip_at(offset), :, d_cols_of(j)],
             dst_ref=back.at[chip, :, d_cols_of(j)],
-            send_sem=bs_sem.at[j],
+            send_sem=send_sem.at[0],
             recv_sem=br_sem.at[j],
             device_id=same_core(offset),
             device_id_type=MESH,
@@ -380,7 +375,7 @@
         return pltpu.make_async_remote_copy(
             src_ref=tail_out.at[t, row_of(device_at(offset))],
             dst_ref=tail.at[t, me],
-            send_sem=ts_sem.at[t],
+            send_sem=send_sem.at[0],
             recv_sem=tr_sem.at[t],
             device_id={"expert": device_at(offset)},
             device_id_type=MESH,
@@ -396,11 +391,11 @@
         tail_copy(t).wait()
         weight = down_buf[0, :, t * t_cols : (t + 1) * t_cols]
         value = jnp.dot(hid[...], weight, preferred_element_type=F32)
+        if t == TAIL_PARTS - 1:
+            add_pair(MAIN_PARTS - 1)
         tail_out[t] = value.astype(BF16).reshape(n, CAP, t_cols)
         each(1, n, lambda o, t=t: tail_send(t, o).start())
         tail_own(t).start()
-        if t == 0:
-            add_pair(MAIN_PARTS - 1)
 
     stat_swap().wait_recv()
     total = stat_pair[0] + stat_pair[1]
@@ -490,17 +485,12 @@
             dma((W_SLOTS,)),
             dma((W_SLOTS,)),
             dma((MAIN_PARTS + TAIL_PARTS,)),
-            dma((K_STEPS,)),
-            dma((K_STEPS,)),
+            dma((1,)),
             dma((K_STEPS,)),
             dma((K_STEPS,)),
             dma((MAIN_PARTS,)),
             dma((MAIN_PARTS,)),
-            dma((MAIN_PARTS,)),
-            dma((MAIN_PARTS,)),
             dma((TAIL_PARTS,)),
-            dma((TAIL_PARTS,)),
-            dma((2,)),
             dma((2,)),
             dma((4,)),
         ],

time: 33.9 us -> 33.6 us (level)
  no operation moved by 1% of the time
where the time goes in v4:
time: 33.6 us; the launch traced here: 33.5 us
  Pallas kernels  32.8 us (98%)
  between operations  0.64 us (2%)
    pallas_call x1, Pallas kernels, local(): pl.pallas_call(functools.partial(kernel, n), out_shape=(pltpu.VMEM((tok_r...  32.2 us

profile of v4, /device:TPU:0, one launch (start us, length us, event | category | flops | bytes accessed | tf_op | source)
XLA Modules:
  0.0 33.5 jit_solution(8184890944006679348)
XLA Ops:
  0.6 32.2 %shard_map.86 = (bf16[4,6144]{1,0:T(4,128)(2,1)S(1)}, f32[1,128]{1,0:T(1,128)S(1)}) custom-call(bf16[4,6144]{1,0:T(4,128)(2,1)} %tok_hbm.1, bf16[4,6144]{1,0:T(4,128)(2,1)} %bitcast.5, s32[2,4]{1,0:T(2,128)} %bitcast.6, s32[2,4]{1,0:T(2,128)} %bitcast.7, bf16[6144,2048]{1,0:T(8,128)(2,1)} %gate_hbm.1, bf16[6144,2048]{1,0:T(8,128)(2,1)} %up_hbm.1, ...), custom_call_target="tpu_custom_call" | custom-call | tf_op jit(solution)/shard_map/pallas_call | solution.py:454
  32.8 0.6 %shard_map.87 = (bf16[4,6144]{1,0:T(4,128)(2,1)}, f32[1,128]{1,0:T(1,128)}) custom-call(bf16[4,6144]{1,0:T(4,128)(2,1)S(1)} %get-tuple-element.6.mixed_ref, f32[1,128]{1,0:T(1,128)S(1)} %get-tuple-element.7.bal_ref), custom_call_target="tpu_custom_call" | custom-call | tf_op jit(solution)/shard_map/pallas_call | solution.py:510
